TPU v7x, 32 devices: a whole 2x2x4 slice. The times are simulated.
32 devices in a mesh: samp: 16 (over z, y, x), tgt: 2 (over core).
Axes of the slice: x: 2, y: 2, z: 4, core: 2. Of those that a mesh axis runs over, the one named last changes fastest.
Arguments:
- samples: bfloat16 [3072, 128], P('samp'), may hold values from -6 to 6
- omega: bfloat16 [128, 4096], replicated, may hold values from -0.5 to 0.5
- phase: float32 [4096], replicated, may hold values from -3.140625 to 3.140625
- right_side: float32 [4096, 512], P('samp', 'tgt'), may hold values from -6 to 6
Outputs:
- weights: float32 [4096, 512], P('samp', 'tgt')
All inputs are finite; a program needn't handle non-finite values.
Results may differ from a plain program's by a relative error of at most 0.011.
The roundings to bfloat16 on the way count: a program that leaves them out, or rounds other values in their place, can miss the bound.
Values may be sent and summed in bfloat16 or wider, within the bound.
A program may use at most 128 MiB of HBM per device.

v0:
```python
import math

import jax
import jax.numpy as jnp
from jax import lax
from jax.sharding import PartitionSpec as P

ITERS = 2


ridge = 1.0


def precise_dot(left_matrix, right_matrix):
    return jnp.dot(left_matrix, right_matrix, precision=lax.Precision.HIGHEST)


def spd_solve(gram_matrix, rhs_matrix):
    factor = jnp.linalg.cholesky(gram_matrix)
    return jax.scipy.linalg.cho_solve((factor, True), rhs_matrix)


def cosine_block(samples, omega, phase, first_row, row_count):
    omega_cols = lax.dynamic_slice_in_dim(omega, first_row, row_count, 1)
    phase_cols = lax.dynamic_slice_in_dim(phase, first_row, row_count, 0)
    preact = jnp.dot(samples, omega_cols, preferred_element_type=jnp.float32) + phase_cols
    return jnp.cos(preact).astype(jnp.bfloat16)


def full_gram(stacked):
    summed = lax.psum(stacked, "samp")
    return lax.all_gather(summed, "tgt", axis=2, tiled=True)


def body(samples, omega, phase, right_side):
    feat_rows, col_count = right_side.shape
    samp_count = lax.axis_size("samp")
    feat_total = omega.shape[1]
    sample_total = samples.shape[0] * samp_count
    col_offset = lax.axis_index("tgt") * col_count
    store_block = math.gcd(feat_total, 512)
    stored = jnp.concatenate(
        [
            cosine_block(samples, omega, phase, index_block * store_block, store_block)
            for index_block in range(feat_total // store_block)
        ],
        axis=1,
    )

    def columns(first_row, row_count):
        return lax.dynamic_slice_in_dim(stored, first_row, row_count, 1)

    resid_all = lax.all_gather(right_side, "tgt", axis=1, tiled=True)
    direction_all = resid_all
    weight_own = jnp.zeros_like(right_side)
    gram_rr = full_gram(precise_dot(resid_all.T, right_side)[None])[0]
    for iteration in range(ITERS):
        direction_own = lax.dynamic_slice_in_dim(direction_all, col_offset, col_count, 1)
        initial = jnp.zeros((samples.shape[0], col_count), jnp.float32)
        shard_piece = lax.all_gather(direction_own.astype(jnp.bfloat16), "samp", axis=0, tiled=True)
        piece_rows = shard_piece.shape[0]
        block_size = math.gcd(piece_rows, 512)

        def project_one_block(index_block, acc_value):
            begin_row = index_block * block_size
            sub_piece = lax.dynamic_slice_in_dim(shard_piece, begin_row, block_size, 0)
            return acc_value + jnp.dot(
                columns(begin_row, block_size), sub_piece, preferred_element_type=jnp.float32
            )

        projected = lax.fori_loop(0, piece_rows // block_size, project_one_block, initial)
        proj_bf = projected.astype(jnp.bfloat16)
        transpose_row_count = feat_rows * lax.axis_size("samp")
        transpose_block_size = math.gcd(transpose_row_count, 512)

        def transpose_one_block(index_block, result):
            begin_row = index_block * transpose_block_size
            feats_block = columns(begin_row, transpose_block_size)
            block_term = lax.dot_general(
                feats_block, proj_bf, (((0,), (0,)), ((), ())), preferred_element_type=jnp.float32
            )
            return lax.dynamic_update_slice_in_dim(result, block_term, begin_row, 0)

        zero_rows = jnp.zeros((transpose_row_count, col_count), jnp.float32)
        summed_image = lax.psum_scatter(
            lax.fori_loop(
                0, transpose_row_count // transpose_block_size, transpose_one_block, zero_rows
            ),
            "samp",
            scatter_dimension=0,
            tiled=True,
        )
        image_own = summed_image / sample_total + ridge * direction_own
        image_all = lax.all_gather(image_own, "tgt", axis=1, tiled=True)
        gram_pq = full_gram(precise_dot(direction_all.T, image_own)[None])[0]
        alpha_coef = spd_solve(gram_pq, gram_rr)
        alpha_own = lax.dynamic_slice_in_dim(alpha_coef, col_offset, col_count, 1)
        weight_own = weight_own + precise_dot(direction_all, alpha_own)
        if iteration + 1 < ITERS:
            resid_all = resid_all - precise_dot(image_all, alpha_coef)
            resid_now = lax.dynamic_slice_in_dim(resid_all, col_offset, col_count, 1)
            gram_new = full_gram(precise_dot(resid_all.T, resid_now)[None])[0]
            beta_coef = spd_solve(gram_rr, gram_new)
            direction_all = resid_all + precise_dot(direction_all, beta_coef)
            gram_rr = gram_new
    return weight_own


def solution(mesh):
    placed = (P("samp", None), P(), P(), P("samp", "tgt"))
    return jax.shard_map(
        body, mesh=mesh, in_specs=placed, out_specs=P("samp", "tgt"), check_vma=False
    )
```

profile of v0, /device:TPU:0, one launch (start us, length us, event | category | flops | bytes accessed | tf_op | source)
XLA Modules:
  0.0 1215.1 jit_solution(10789328759363507932)
XLA Ops:
  22.8 50.4 %all-gather.7.cloned.1.call-done = bf16[4096,256]{1,0:T(8,128)(2,1)} async-done(((bf16[256,256]{1,0:T(8,128)(2,1)}), bf16[4096,256]{1,0:T(8,128)(2,1)}) %all-gather.7.cloned.1.call-update) | async-done | bytes 2097168 | tf_op jit(solution)/shard_map/all_gather | solution.py:60
  96.3 91.8 %reduce-scatter.3.cloned.1.call-done = f32[256,256]{1,0:T(8,128)} async-done(((f32[4096,256]{1,0:T(8,128)}), f32[256,256]{1,0:T(8,128)}) %reduce-scatter.3.cloned.1.call-update) | async-done | bytes 262160 | tf_op jit(solution)/shard_map/reduce_scatter | solution.py:85
  190.6 114.9 %all-reduce.10.cloned.1.call-done = (f32[1,512,256]{1,2,0:T(8,128)}, f32[1,512,256]{1,2,0:T(8,128)}) async-done(((f32[1,512,256]{1,2,0:T(8,128)}, f32[1,512,256]{1,2,0:T(8,128)}), (f32[1,512,256]{1,2,0:T(8,128)}, f32[1,512,256]{1,2,0:T(8,128)})) %all-reduce.10.cloned.1.call-update) | async-done | bytes 1048592 | tf_op jit(solution)/shard_map/psum | solution.py:31
  320.1 11.7 cholesky.374
  332.0 9.8 custom-call.35
  344.3 11.7 cholesky.393
  356.1 10.0 custom-call.36
  367.6 11.7 cholesky.414
  391.3 11.7 cholesky.431
  408.6 12.0 while.64
  420.6 39.3 %custom-call.38 = f32[4,128,128]{1,2,0:T(8,128)S(1)} custom-call(f32[4,128,128]{2,1,0:T(8,128)S(1)} %get-tuple-element.377), custom_call_target="InvertDiagBlocksLowerTriangular" | custom-call | tf_op jit(solution)/shard_map/jit(_cho_solve)/triangular_solve | solution.py:20
  475.0 11.7 cholesky.446
  487.5 10.8 custom-call.39
  502.1 12.5 %cholesky.465 = f32[128,128]{1,0:T(8,128)S(1)} custom-call(f32[128,128]{1,0:T(8,128)} %cholesky.603), custom_call_target="Cholesky" | custom-call | tf_op jit(solution)/shard_map/jit(cholesky)/cholesky | solution.py:19
  515.3 10.6 custom-call.40
  529.1 12.5 %cholesky.486 = f32[128,128]{1,0:T(8,128)} custom-call(f32[128,128]{1,0:T(8,128)S(1)} %cholesky.608), custom_call_target="Cholesky" | custom-call | tf_op jit(solution)/shard_map/jit(cholesky)/cholesky | solution.py:19
  543.1 10.4 custom-call.41
  555.9 12.3 %cholesky.503 = f32[128,128]{1,0:T(8,128)} custom-call(f32[128,128]{1,0:T(8,128)S(1)} %convolution_subtract_fusion.26), custom_call_target="Cholesky" | custom-call | tf_op jit(solution)/shard_map/jit(cholesky)/cholesky | solution.py:19
  578.3 105.3 %all-reduce.6.cloned.1.call-done = f32[1,512,256]{2,1,0:T(8,128)} async-done(((f32[1,512,256]{2,1,0:T(8,128)}), f32[1,512,256]{2,1,0:T(8,128)}) %all-reduce.6.cloned.1.call-update) | async-done | bytes 524304 | tf_op jit(solution)/shard_map/psum | solution.py:31
  684.4 14.8 %while.65 = (s32[]{:T(128)}, f32[512,512]{1,0:T(8,128)}, s32[4,2]{0,1:T(2,128)S(1)}, f32[4,128,128]{2,1,0:T(8,128)}, s32[]{:T(128)}) while((s32[]{:T(128)}, f32[512,512]{1,0:T(8,128)}, s32[4,2]{0,1:T(2,128)S(1)}, f32[4,128,128]{2,1,0:T(8,128)}, s32[]{:T(128)}) %tuple.227), condition=%wide.while_cond.clone, body=%wide.while_body.clone.sunk | while | flops 2 | bytes 132705 | solution.py:20
  699.2 40.8 %custom-call.42 = f32[4,128,128]{1,2,0:T(8,128)} custom-call(f32[4,128,128]{2,1,0:T(8,128)} %get-tuple-element.378), custom_call_target="InvertDiagBlocksLowerTriangular" | custom-call | tf_op jit(solution)/shard_map/jit(_cho_solve)/triangular_solve | solution.py:20
  752.9 59.5 %all-gather.15.cloned.1.call-done = bf16[4096,256]{1,0:T(8,128)(2,1)} async-done(((bf16[256,256]{1,0:T(8,128)(2,1)}), bf16[4096,256]{1,0:T(8,128)(2,1)}) %all-gather.15.cloned.1.call-update) | async-done | bytes 2097168 | tf_op jit(solution)/shard_map/all_gather | solution.py:60
  833.1 94.1 %reduce-scatter.5.cloned.1.call-done = f32[256,256]{1,0:T(8,128)} async-done(((f32[4096,256]{1,0:T(8,128)}), f32[256,256]{1,0:T(8,128)}) %reduce-scatter.5.cloned.1.call-update) | async-done | bytes 262160 | tf_op jit(solution)/shard_map/reduce_scatter | solution.py:85
  929.9 111.0 %all-reduce.8.cloned.1.call-done = f32[1,512,256]{1,2,0:T(8,128)} async-done(((f32[1,512,256]{1,2,0:T(8,128)}), f32[1,512,256]{1,2,0:T(8,128)}) %all-reduce.8.cloned.1.call-update) | async-done | bytes 524304 | tf_op jit(solution)/shard_map/psum | solution.py:31
  1055.6 11.7 cholesky.518
  1067.5 9.8 custom-call.43
  1079.8 11.7 cholesky.537
  1092.9 10.0 custom-call.44
  1104.4 11.7 cholesky.558
  1128.1 11.7 cholesky.575
  1144.4 11.5 while.66
  1155.9 39.3 %custom-call.46 = f32[4,128,128]{1,2,0:T(8,128)S(1)} custom-call(f32[4,128,128]{2,1,0:T(8,128)S(1)} %get-tuple-element.379), custom_call_target="InvertDiagBlocksLowerTriangular" | custom-call | tf_op jit(solution)/shard_map/jit(_cho_solve)/triangular_solve | solution.py:20
  (292 shorter events, 267.8 us)
Async XLA Ops:
  6.5 4.2 copy-start
  6.5 6.5 copy-start.26
  6.5 66.7 %all-gather.7.cloned.1.call-start = ((), (), s32[]{:S(2)}) async-start(), calls=%async_computation.2 | async-start | bytes 2228224 | tf_op jit(solution)/shard_map/all_gather | solution.py:60
  9.9 178.2 %reduce-scatter.3.cloned.1.call-start = ((), (), s32[]{:S(2)}) async-start(), calls=%async_computation.3 | async-start | bytes 4456448 | tf_op jit(solution)/shard_map/reduce_scatter | solution.py:85
  93.9 211.5 %all-reduce.10.cloned.1.call-start = ((), (), s32[]{:S(2)}) async-start(), calls=%async_computation.12 | async-start | bytes 2097152 | tf_op jit(solution)/shard_map/psum | solution.py:31
  190.5 124.4 %all-gather.9.cloned.1.call-start = ((), (), s32[]{:S(2)}) async-start(), calls=%async_computation.4 | async-start | bytes 1572864 | tf_op jit(solution)/shard_map/all_gather | solution.py:32
  305.5 154.5 %all-gather.11.cloned.1.call-start = ((), (), s32[]{:S(2)}) async-start(), calls=%async_computation.5 | async-start | bytes 1572864 | tf_op jit(solution)/shard_map/all_gather | solution.py:32
  307.8 375.8 %all-reduce.6.cloned.1.call-start = ((), (), s32[]{:S(2)}) async-start(), calls=%async_computation.6 | async-start | bytes 1048576 | tf_op jit(solution)/shard_map/psum | solution.py:31
  315.0 2.7 copy-start.9
  319.1 1.0 copy-start.15
  459.9 7.9 copy-start.20
  460.0 2.7 copy-start.1
  462.6 2.3 copy-start.7
  468.2 3.4 copy-start.21
  471.2 1.6 copy-start.2
  471.7 2.2 copy-start.10
  472.0 2.0 copy-start.12
  568.2 7.6 copy-start.25
  573.2 166.8 %all-gather.13.cloned.1.call-start = ((), (), s32[]{:S(2)}) async-start(), calls=%async_computation.7 | async-start | bytes 1572864 | tf_op jit(solution)/shard_map/all_gather | solution.py:32
  683.6 128.7 %all-gather.15.cloned.1.call-start = ((), (), s32[]{:S(2)}) async-start(), calls=%async_computation.8 | async-start | bytes 2228224 | tf_op jit(solution)/shard_map/all_gather | solution.py:60
  699.2 44.9 %copy-start.6 = (f32[512,512]{1,0:T(8,128)S(1)}, f32[512,512]{1,0:T(8,128)}, u32[]{:S(2)}) copy-start(f32[512,512]{1,0:T(8,128)} %get-tuple-element.842) | copy-start | bytes 3145732
  740.0 5.5 copy-start.22
  749.6 1.4 copy-start.5
  752.8 174.4 %reduce-scatter.5.cloned.1.call-start = ((), (), s32[]{:S(2)}) async-start(), calls=%async_computation.9 | async-start | bytes 4456448 | tf_op jit(solution)/shard_map/reduce_scatter | solution.py:85
  833.0 207.9 %copy-start.3 = (f32[128,512]{1,0:T(8,128)S(1)}, f32[128,512]{1,0:T(8,128)}, u32[]{:S(2)}) copy-start(f32[128,512]{1,0:T(8,128)} %copy-done.2) | copy-start | bytes 786436
  833.0 207.9 %copy-start.13 = (f32[128,512]{1,0:T(8,128)S(1)}, f32[128,512]{1,0:T(8,128)}, u32[]{:S(2)}) copy-start(f32[128,512]{1,0:T(8,128)} %copy-done.12) | copy-start | bytes 786436
  833.0 207.9 %copy-start.18 = (f32[128,512]{1,0:T(8,128)S(1)}, f32[128,512]{1,0:T(8,128)}, u32[]{:S(2)}) copy-start(f32[128,512]{1,0:T(8,128)} %fusion.170) | copy-start | bytes 786436
  833.0 207.9 %all-reduce.8.cloned.1.call-start = ((), (), s32[]{:S(2)}) async-start(), calls=%async_computation.10 | async-start | bytes 1048576 | tf_op jit(solution)/shard_map/psum | solution.py:31
  929.7 120.8 %all-gather.17.cloned.1.call-start = ((), (), s32[]{:S(2)}) async-start(), calls=%async_computation.11 | async-start | bytes 1572864 | tf_op jit(solution)/shard_map/all_gather | solution.py:32
  1050.5 2.7 copy-start.11
  1155.9 42.5 %copy-start.8 = (f32[512,512]{1,0:T(8,128)S(1)}, f32[512,512]{1,0:T(8,128)}, u32[]{:S(2)}) copy-start(f32[512,512]{1,0:T(8,128)} %get-tuple-element.844) | copy-start | bytes 3145732
  1204.9 1.4 copy-start.17
  (6 other events, 5.1 us)
Sparse Core Ops, SparseCore 0:
  10.1 63.1 all-gather.6
  94.0 94.0 reduce-scatter.2
  193.4 111.9 all-reduce.9
  306.8 8.0 all-gather.8
  316.4 10.1 all-gather.10
  573.3 110.2 all-reduce.5
  685.2 8.0 all-gather.12
  752.9 59.3 all-gather.14
  833.1 94.0 reduce-scatter.4
  932.2 108.6 all-reduce.7
  1042.4 8.0 all-gather.16
where the time goes:
time: 1230 us; the launch traced here: 1220 us
  waiting for transfers between devices  643 us (52%)
  other arithmetic  372 us (30%)
  matrix products  111 us (9%)
  local copies, waits for them, and re-layouts  60.6 us (5%)
  between operations  22.3 us (2%)
    psum x3, waiting for transfers between devices, full_gram(): summed = lax.psum(stacked, 'samp')  331 us
    another operation x43, other arithmetic, spd_solve(): factor = jnp.linalg.cholesky(gram_matrix)  243 us
    reduce_scatter x2, waiting for transfers between devices, body(): lax.psum_scatter(lax.fori_loop(0, transpose_row_count // transpose_block_...  186 us
    another operation x8, other arithmetic, spd_solve(): return jax.scipy.linalg.cho_solve((factor, True), rhs_matrix)  124 us
    all_gather x2, waiting for transfers between devices, body(): lax.all_gather(direction_own.astype(jnp.bfloat16), 'samp', axis=0, tiled=...  110 us
    another operation x40, local copies, waits for them, and re-layouts, spd_solve(): return jax.scipy.linalg.cho_solve((factor, True), rhs_matrix)  38.5 us
    another operation x42, matrix products, spd_solve(): return jax.scipy.linalg.cho_solve((factor, True), rhs_matrix)  31.8 us
  transfers between devices with their start and end apart: 11, of which 9 were waited for; matrix products, arithmetic and copies ran while one was open for 18% of the time, Pallas kernels for 0%

commit v1 on v0

v1 whole, which is shorter than its diff:
```python
import jax
import jax.numpy as jnp
from jax import lax
from jax.experimental import pallas as pl
from jax.experimental.pallas import tpu as pltpu
from jax.sharding import PartitionSpec as P

ridge = 1.0
HI = lax.Precision.HIGHEST
F32 = jnp.float32
BF16 = jnp.bfloat16
BLOCK = 128
GROUP = 4


def precise_dot(left_matrix, right_matrix):
    return jnp.dot(left_matrix, right_matrix, precision=HI, preferred_element_type=F32)


def gram_dot(left_matrix, right_matrix):
    return lax.dot_general(
        left_matrix, right_matrix, (((0,), (0,)), ((), ())), precision=HI, preferred_element_type=F32
    )


def cosine(x):
    n = jnp.round(x * 0.3183098861837907)
    r = x - n * 3.140625
    r = r - n * 9.67025756835938e-4
    r = r - n * 6.2771141529083251953e-7
    half = n * 0.5
    sign = 1.0 - 4.0 * (half - jnp.floor(half))
    s = r * r
    p = 2.08767569878681e-9
    for coef in (
        -2.755731922398589e-7,
        2.48015873015873e-5,
        -1.388888888888889e-3,
        4.166666666666667e-2,
        -0.5,
        1.0,
    ):
        p = p * s + coef
    return p * sign


def invert_small(pivots):
    size = len(pivots)
    held = [list(line) for line in pivots]
    for j in range(size):
        inverse = 1.0 / held[j][j]
        line = [inverse if m == j else held[j][m] * inverse for m in range(size)]
        for i in range(size):
            if i != j:
                factor = held[i][j]
                held[i] = [
                    -factor * line[m] if m == j else held[i][m] - factor * line[m] for m in range(size)
                ]
        held[j] = line
    return held


def invert_blocks(values):
    size = values[0].shape[0]
    many = [[value[t * 8 : t * 8 + 8, :] for t in range(size // 8)] for value in values]
    lane = lax.broadcasted_iota(jnp.int32, (8, size), 1)
    sub = lax.broadcasted_iota(jnp.int32, (8, size), 0)
    for j in range(0, size, GROUP):
        home, inner = divmod(j, 8)
        in_group = (lane >= j) & (lane < j + GROUP)
        for which, tiles in enumerate(many):
            rows = [
                jnp.broadcast_to(tiles[home][inner + k : inner + k + 1, :], (8, size)) for k in range(GROUP)
            ]
            pivots = invert_small(
                [[jnp.broadcast_to(row[:, j + m : j + m + 1], (8, size)) for m in range(GROUP)] for row in rows]
            )
            scaled = []
            for k in range(GROUP):
                line = pivots[k][0] * rows[0]
                for m in range(1, GROUP):
                    line = line + pivots[k][m] * rows[m]
                for m in range(GROUP):
                    line = jnp.where(lane == j + m, pivots[k][m], line)
                scaled.append(line)
            nxt = []
            for t, tile in enumerate(tiles):
                new = jnp.where(in_group, 0.0, tile)
                for k in range(GROUP):
                    new = new - jnp.broadcast_to(tile[:, j + k : j + k + 1], (8, size)) * scaled[k]
                if t == home:
                    for k in range(GROUP):
                        new = jnp.where(sub == inner + k, scaled[k], new)
                nxt.append(new)
            many[which] = nxt
    return [jnp.concatenate(tiles, axis=0) for tiles in many]


def spd_kernel(gram_ref, rhs_ref, out_ref, work):
    systems, total = gram_ref.shape[:2]
    size = BLOCK
    work[...] = gram_ref[...]
    out_ref[...] = rhs_ref[...]

    def step(k, carry):
        at = pl.ds(pl.multiple_of(k * size, size), size)
        inverses = invert_blocks([work[s, at, at] for s in range(systems)])
        for s in range(systems):
            inv = inverses[s]
            row_a = precise_dot(inv, work[s, at, :])
            row_x = precise_dot(inv, out_ref[s, at, :])
            for i in range(total // size):
                rows = pl.ds(i * size, size)
                left = jnp.where(k == i, 0.0, work[s, rows, at])
                work[s, rows, :] = work[s, rows, :] - precise_dot(left, row_a)
                out_ref[s, rows, :] = out_ref[s, rows, :] - precise_dot(left, row_x)
            work[s, at, :] = row_a
            out_ref[s, at, :] = row_x
        return carry

    lax.fori_loop(0, total // size, step, 0)


def spd_solve(gram_matrices, rhs_matrices):
    systems, total, cols = rhs_matrices.shape
    return pl.pallas_call(
        spd_kernel,
        out_shape=jax.ShapeDtypeStruct((systems, total, cols), F32),
        in_specs=[pl.BlockSpec(memory_space=pltpu.VMEM)] * 2,
        out_specs=pl.BlockSpec(memory_space=pltpu.VMEM),
        scratch_shapes=[pltpu.VMEM((systems, total, total), F32)],
        compiler_params=pltpu.CompilerParams(vmem_limit_bytes=24 * 2**20),
        cost_estimate=pl.CostEstimate(flops=2 * 10**10, bytes_accessed=3 * 2**20, transcendentals=0),
        name="spd",
    )(gram_matrices, rhs_matrices)


def full_gram(piece):
    summed = lax.psum(piece, "samp")
    return lax.all_gather(summed, "tgt", axis=1, tiled=True)


def body(samples, omega, phase, right_side):
    col_count = right_side.shape[1]
    sample_total = samples.shape[0] * lax.axis_size("samp")
    col_offset = lax.axis_index("tgt") * col_count

    def own(matrix):
        return lax.dynamic_slice_in_dim(matrix, col_offset, col_count, 1)

    def wide(matrix):
        return lax.all_gather(matrix, "tgt", axis=1, tiled=True)

    right_cols = lax.all_gather(right_side.astype(BF16), "samp", axis=0, tiled=True)
    right_all = wide(right_side)
    gram_rr = full_gram(gram_dot(right_all, right_side))
    feats = cosine(jnp.dot(samples, omega, preferred_element_type=F32) + phase).astype(BF16)

    projected = jnp.dot(feats, right_cols, preferred_element_type=F32).astype(BF16)
    lifted = lax.dot_general(feats, projected, (((0,), (0,)), ((), ())), preferred_element_type=F32)
    lifted_own = lax.psum_scatter(lifted, "samp", scatter_dimension=0, tiled=True) / sample_total
    proj_all = wide(projected)
    gram_py = full_gram(
        lax.dot_general(proj_all, projected, (((0,), (0,)), ((), ())), preferred_element_type=F32)
    )
    gram_pq = gram_py / sample_total + ridge * gram_rr
    unit = jnp.eye(gram_rr.shape[0], dtype=F32)
    solved = spd_solve(jnp.stack([gram_pq, gram_rr]), jnp.stack([gram_rr, unit]))
    alpha, gram_inverse = solved[0], solved[1]

    lifted_all = wide(lifted_own)
    resid_all = right_all - precise_dot(lifted_all + ridge * right_all, alpha)
    resid_own = own(resid_all)
    resid_cols = lax.all_gather(resid_own.astype(BF16), "samp", axis=0, tiled=True)
    gram_new = full_gram(gram_dot(resid_all, resid_own))
    beta = precise_dot(gram_inverse, gram_new)
    direction_all = resid_all + precise_dot(right_all, beta)
    carried = precise_dot(proj_all.astype(F32), own(beta))

    second = (jnp.dot(feats, resid_cols, preferred_element_type=F32) + carried).astype(BF16)
    gram_two = full_gram(
        lax.dot_general(wide(second), second, (((0,), (0,)), ((), ())), preferred_element_type=F32)
        / sample_total
        + ridge * gram_dot(direction_all, own(direction_all))
    )
    alpha_two = spd_solve(gram_two[None], own(gram_new)[None])[0]
    return precise_dot(right_all, own(alpha)) + precise_dot(direction_all, alpha_two)


def solution(mesh):
    placed = (P("samp", None), P(), P(), P("samp", "tgt"))
    return jax.shard_map(
        body, mesh=mesh, in_specs=placed, out_specs=P("samp", "tgt"), check_vma=False
    )
```

time: 1230 us -> 680 us (0.55); the launches traced: 1220 us -> 680 us
  other arithmetic: 372 us -> 5.25 us
  waiting for transfers between devices: 643 us -> 514 us
  Pallas kernels: 0 us -> 101 us
  matrix products: 111 us -> 29.2 us
  local copies, waits for them, and re-layouts: 60.6 us -> 7.27 us
    another operation x51 -> x2, other arithmetic: 368 us -> 2.46 us  [the longest x1 1.76 us: body(): jnp.stack([gram_pq, gram_rr])]
    reduce_scatter x2 -> x1, waiting for transfers between devices: 186 us -> 39.1 us  [body(): lax.psum_scatter(lifted, 'samp', scatter_dimension=0, tiled=True)]
    pallas_call x0 -> x2, Pallas kernels: none -> 101 us  [spd_solve(): pl.pallas_call(spd_kernel, out_shape=jax.ShapeDtypeStruct((systems, total...]
    another operation x60 -> x0, matrix products: 50 us -> none  [the longest x42 31.8 us: spd_solve(): return jax.scipy.linalg.cho_solve((factor, True), rhs_matrix)]
    another operation x54 -> x0, local copies, waits for them, and re-layouts: 43.9 us -> none  [the longest x40 38.5 us: spd_solve(): return jax.scipy.linalg.cho_solve((factor, True), rhs_matrix)]
    dot_general x48 -> x15, matrix products: 60.9 us -> 29.2 us  [the longest x6 8.9 us: precise_dot(): jnp.dot(left_matrix, right_matrix, precision=HI, preferred_element_type=F32)]
    all_gather x6, waiting for transfers between devices: 126 us -> 146 us  [the longest x1 57.4 us: body(): lax.all_gather(resid_own.astype(BF16), 'samp', axis=0, tiled=True)]
  transfers between devices with their start and end apart: 11 -> 10, of which waited for: 9 -> 10; matrix products, arithmetic and copies ran while one was open for 18% -> 3% of each run, Pallas kernels for 0% -> 8%
where the time goes in v1:
time: 680 us
  waiting for transfers between devices  514 us (76%)
  Pallas kernels  101 us (15%)
  matrix products  29.2 us (4%)
  between operations  13.8 us (2%)
  blocking collectives  8.81 us (1%)
  local copies, waits for them, and re-layouts  7.27 us (1%)
    psum x3, waiting for transfers between devices, full_gram(): summed = lax.psum(piece, 'samp')  328 us
    pallas_call x2, Pallas kernels, spd_solve(): pl.pallas_call(spd_kernel, out_shape=jax.ShapeDtypeStruct((systems, total...  101 us
    all_gather x1, waiting for transfers between devices, body(): lax.all_gather(resid_own.astype(BF16), 'samp', axis=0, tiled=True)  57.4 us
    all_gather x1, waiting for transfers between devices, body(): lax.all_gather(right_side.astype(BF16), 'samp', axis=0, tiled=True)  54.7 us
    reduce_scatter x1, waiting for transfers between devices, body(): lax.psum_scatter(lifted, 'samp', scatter_dimension=0, tiled=True)  39.1 us
    all_gather x4, waiting for transfers between devices, full_gram(): return lax.all_gather(summed, 'tgt', axis=1, tiled=True)  33.9 us
  transfers between devices with their start and end apart: 10, of which 10 were waited for; matrix products, arithmetic and copies ran while one was open for 3% of the time, Pallas kernels for 8%

profile of v1, /device:TPU:0, one launch (start us, length us, event | category | flops | bytes accessed | tf_op | source)
XLA Modules:
  0.0 679.9 jit_solution(583211343718142061)
XLA Ops:
  6.5 1.7 convert_element_type.27
  8.3 2.5 all_gather.33
  11.7 2.8 fusion.27
  14.4 4.1 fusion.3
  18.6 54.7 %all-gather.7.cloned.1.call-done = bf16[4096,256]{1,0:T(8,128)(2,1)} async-done(((bf16[256,256]{1,0:T(8,128)(2,1)}), bf16[4096,256]{1,0:T(8,128)(2,1)}) %all-gather.7.cloned.1.call-update) | async-done | bytes 2097168 | tf_op jit(solution)/shard_map/all_gather | solution.py:154
  73.2 2.2 convolution_convert_fusion
  75.4 1.9 all_gather.31
  78.5 111.3 %all-reduce.9.cloned.1.call-done = (f32[512,256]{1,0:T(8,128)}, f32[512,256]{1,0:T(8,128)}) async-done(((f32[512,256]{1,0:T(8,128)}, f32[512,256]{1,0:T(8,128)}), (f32[512,256]{1,0:T(8,128)}, f32[512,256]{1,0:T(8,128)})) %all-reduce.9.cloned.1.call-update) | async-done | bytes 1048592 | tf_op jit(solution)/shard_map/psum | solution.py:139
  190.5 2.7 fusion.28
  193.4 6.1 all-gather.11.cloned.1.call-done
  199.5 11.6 %all-gather.9.cloned.1.call-done = f32[512,512]{1,0:T(8,128)} async-done(((f32[512,256]{1,0:T(8,128)}), f32[512,512]{1,0:T(8,128)}) %all-gather.9.cloned.1.call-update) | async-done | bytes 1048592 | tf_op jit(solution)/shard_map/all_gather | solution.py:140
  211.2 1.8 add_bitcast_fusion
  213.7 57.0 %spd.2 = f32[2,512,512]{2,1,0:T(8,128)S(1)} custom-call(f32[2,512,512]{2,1,0:T(8,128)S(1)} %get-tuple-element.8.gram_ref, f32[2,512,512]{2,1,0:T(8,128)S(1)} %get-tuple-element.7.rhs_ref), custom_call_target="tpu_custom_call" | custom-call | flops 20000000000 | bytes 3145728 | tf_op jit(solution)/shard_map/spd/pallas_call | solution.py:126
  270.7 39.1 %reduce-scatter.2.cloned.1.call-done = f32[256,256]{1,0:T(8,128)} async-done(((f32[4096,256]{1,0:T(8,128)}), f32[256,256]{1,0:T(8,128)}) %reduce-scatter.2.cloned.1.call-update) | async-done | bytes 262160 | tf_op jit(solution)/shard_map/reduce_scatter | solution.py:161
  310.7 2.4 all_gather.35
  313.1 2.3 convolution_subtract_fusion
  316.2 1.8 fusion.19
  318.1 108.7 %all-reduce.5.cloned.1.call-done = f32[512,256]{1,0:T(8,128)} async-done(((f32[512,256]{1,0:T(8,128)}), f32[512,256]{1,0:T(8,128)}) %all-reduce.5.cloned.1.call-update) | async-done | bytes 524304 | tf_op jit(solution)/shard_map/psum | solution.py:139
  426.9 1.6 dynamic-slice_convert_fusion
  428.6 7.8 %all-gather.13.cloned.1.call-done = f32[512,512]{1,0:T(8,128)} async-done(((f32[512,256]{1,0:T(8,128)}), f32[512,512]{1,0:T(8,128)}) %all-gather.13.cloned.1.call-update) | async-done | bytes 1048592 | tf_op jit(solution)/shard_map/all_gather | solution.py:140
  436.4 3.1 fusion.8
  439.6 1.1 fusion.4
  441.5 1.8 fusion.17
  443.3 57.4 %all-gather.15.cloned.1.call-done = bf16[4096,256]{1,0:T(8,128)(2,1)} async-done(((bf16[256,256]{1,0:T(8,128)(2,1)}), bf16[4096,256]{1,0:T(8,128)(2,1)}) %all-gather.15.cloned.1.call-update) | async-done | bytes 2097168 | tf_op jit(solution)/shard_map/all_gather | solution.py:174
  500.8 2.8 fusion.29
  503.9 1.9 all_gather.38
  505.9 1.1 fusion.5
  507.3 107.7 %all-reduce.7.cloned.1.call-done = f32[512,256]{1,0:T(8,128)} async-done(((f32[512,256]{1,0:T(8,128)}), f32[512,256]{1,0:T(8,128)}) %all-reduce.7.cloned.1.call-update) | async-done | bytes 524304 | tf_op jit(solution)/shard_map/psum | solution.py:139
  615.0 1.1 dynamic-slice_bitcast_fusion.rhs_ref
  616.1 8.3 %all-gather.17.cloned.1.call-done = f32[512,512]{1,0:T(8,128)} async-done(((f32[512,256]{1,0:T(8,128)}), f32[512,512]{1,0:T(8,128)}) %all-gather.17.cloned.1.call-update) | async-done | bytes 1048592 | tf_op jit(solution)/shard_map/all_gather | solution.py:140
  624.5 1.2 copy-done.2
  625.7 44.5 %spd.3 = f32[1,512,256]{2,1,0:T(8,128)S(1)} custom-call(f32[1,512,512]{2,1,0:T(8,128)S(1)} %bitcast.48, f32[1,512,256]{2,1,0:T(8,128)S(1)} %dynamic-slice_bitcast_fusion.rhs_ref), custom_call_target="tpu_custom_call" | custom-call | flops 20000000000 | bytes 3145728 | tf_op jit(solution)/shard_map/spd/pallas_call | solution.py:126
  (59 shorter events, 9.9 us)
Async XLA Ops:
  6.5 7.9 %copy-start = (bf16[128,4096]{1,0:T(8,128)(2,1)S(1)}, bf16[128,4096]{1,0:T(8,128)(2,1)}, u32[]{:S(2)}) copy-start(bf16[128,4096]{1,0:T(8,128)(2,1)} %param.5) | copy-start | bytes 3145732
  6.5 66.7 %all-gather.7.cloned.1.call-start = ((), (), s32[]{:S(2)}) async-start(), calls=%async_computation.1 | async-start | bytes 2228224 | tf_op jit(solution)/shard_map/all_gather | solution.py:154
  8.3 181.6 %all-reduce.9.cloned.1.call-start = ((), (), s32[]{:S(2)}) async-start(), calls=%async_computation.10 | async-start | bytes 2097152 | tf_op jit(solution)/shard_map/psum | solution.py:139
  10.8 0.8 copy-start.4
  18.6 171.9 %copy-start.3 = (bf16[192,4096]{1,0:T(8,128)(2,1)}, bf16[192,4096]{1,0:T(8,128)(2,1)S(1)}, u32[]{:S(2)}) copy-start(bf16[192,4096]{1,0:T(8,128)(2,1)S(1)} %fusion.3) | copy-start | bytes 4718596
  78.5 121.1 %all-gather.11.cloned.1.call-start = ((), (), s32[]{:S(2)}) async-start(), calls=%async_computation.3 | async-start | bytes 1572864 | tf_op jit(solution)/shard_map/all_gather | solution.py:140
  189.9 21.3 %all-gather.9.cloned.1.call-start = ((), (), s32[]{:S(2)}) async-start(), calls=%async_computation.2 | async-start | bytes 1572864 | tf_op jit(solution)/shard_map/all_gather | solution.py:140
  190.4 119.3 %reduce-scatter.2.cloned.1.call-start = ((), (), s32[]{:S(2)}) async-start(), calls=%async_computation.4 | async-start | bytes 4456448 | tf_op jit(solution)/shard_map/reduce_scatter | solution.py:161
  193.3 233.5 %all-reduce.5.cloned.1.call-start = ((), (), s32[]{:S(2)}) async-start(), calls=%async_computation.5 | async-start | bytes 1048576 | tf_op jit(solution)/shard_map/psum | solution.py:139
  199.5 13.4 %copy-start.13 = (f32[512,512]{1,0:T(8,128)S(1)}, f32[512,512]{1,0:T(8,128)}, u32[]{:S(2)}) copy-start(f32[512,512]{1,0:T(8,128)} %all-gather.11.cloned.1.call-done) | copy-start | bytes 3145732
  270.6 344.4 %copy-start.1 = (f32[2,512,512]{2,1,0:T(8,128)}, f32[2,512,512]{2,1,0:T(8,128)S(1)}, u32[]{:S(2)}) copy-start(f32[2,512,512]{2,1,0:T(8,128)S(1)} %spd.2) | copy-start | bytes 6291460
  315.4 0.8 copy-start.9
  318.0 118.4 %all-gather.13.cloned.1.call-start = ((), (), s32[]{:S(2)}) async-start(), calls=%async_computation.6 | async-start | bytes 1572864 | tf_op jit(solution)/shard_map/all_gather | solution.py:140
  426.8 73.9 %all-gather.15.cloned.1.call-start = ((), (), s32[]{:S(2)}) async-start(), calls=%async_computation.7 | async-start | bytes 2228224 | tf_op jit(solution)/shard_map/all_gather | solution.py:174
  428.5 186.5 %all-reduce.7.cloned.1.call-start = ((), (), s32[]{:S(2)}) async-start(), calls=%async_computation.8 | async-start | bytes 1048576 | tf_op jit(solution)/shard_map/psum | solution.py:139
  436.4 3.2 copy-start.5
  436.4 3.2 copy-start.10
  439.6 1.1 copy-start.7
  440.7 0.8 copy-start.11
  500.8 2.8 copy-start.8
  500.8 5.1 copy-start.14
  507.0 117.5 %all-gather.17.cloned.1.call-start = ((), (), s32[]{:S(2)}) async-start(), calls=%async_computation.9 | async-start | bytes 1572864 | tf_op jit(solution)/shard_map/all_gather | solution.py:140
  624.5 1.2 copy-start.2
  625.7 44.5 %copy-start.12 = (f32[256,512]{1,0:T(8,128)S(1)}, f32[256,512]{1,0:T(8,128)}, u32[]{:S(2)}) copy-start(f32[256,512]{1,0:T(8,128)} %copy-done.11) | copy-start | bytes 1572868
  625.7 45.5 %slice-start = ((f32[2,512,512]{2,1,0:T(8,128)}), f32[1,512,512]{2,1,0:T(8,128)S(1)}, s32[]{:S(2)}) async-start(f32[2,512,512]{2,1,0:T(8,128)} %copy-done.1), calls=%async_computation.11 | async-start | bytes 2097152 | tf_op jit(solution)/shard_map/slice | solution.py:169
  625.7 45.5 %copy-start.6 = (f32[256,512]{1,0:T(8,128)S(1)}, f32[256,512]{1,0:T(8,128)}, u32[]{:S(2)}) copy-start(f32[256,512]{1,0:T(8,128)} %copy-done.4) | copy-start | bytes 1572868
Sparse Core Ops, SparseCore 0:
  10.1 63.0 all-gather.6
  78.6 111.2 all-reduce.8
  191.4 8.0 all-gather.10
  200.9 10.1 all-gather.8
  213.3 96.3 reduce-scatter.1
  318.1 108.6 all-reduce.4
  428.3 8.0 all-gather.12
  439.2 61.5 all-gather.14
  507.1 107.8 all-reduce.6
  616.4 8.0 all-gather.16
